TPU v7x, 32 devices: a whole 2x2x4 slice. The times are simulated.
32 devices in a mesh: groups: 2 (over y), expert: 8 (over z, core), dp: 2 (over x).
Axes of the slice: x: 2, y: 2, z: 4, core: 2. Of those that a mesh axis runs over, the one named last changes fastest.
Arguments:
- tokens: bfloat16 [1024, 2048], P(('groups', 'expert'), 'dp'), parts along dimension 0, may hold values from -6 to 6
- expert_ids: int32 [1024, 8], P(('groups', 'expert')), parts along dimension 0, may hold values from 0 to 15, all different within a row; in each aligned block of 64 rows (0 to 63, 64 to 127, ...) at most 64 rows name the same one
- gate_levels: int32 [1024, 8], P(('groups', 'expert')), parts along dimension 0, may hold values from 1 to 255
- gate_weight: bfloat16 [16, 2048, 1536], P('expert', None, 'dp'), may hold values from -0.125 to 0.125
- up_weight: bfloat16 [16, 2048, 1536], P('expert', None, 'dp'), may hold values from -0.125 to 0.125
- down_weight: bfloat16 [16, 1536, 2048], P('expert', None, 'dp'), may hold values from -0.15625 to 0.15625
Outputs:
- mixed: bfloat16 [1024, 2048], P(('groups', 'expert'), 'dp'), parts along dimension 0
There are 2 independent parts, one for each index of `groups`. A program takes and returns all parts, laid end to end along the dimension named above; an argument that names none is the same for every part. Nothing has to cross between parts.
Inputs may be any that keep to these rules, and one draw needn't show every extreme that they name: `expert_ids`: each row names 8 different experts. Among the rows of one index of the expert axis no expert is named more than 64 times, a bound that some block reaches.
All inputs are finite; a program needn't handle non-finite values.
Results may differ from a plain program's by a relative error of at most 0.0057.
Values may be sent and summed in bfloat16 or wider, within the bound.
A program may use at most 64 MiB of HBM per device.

v0:
```python
import jax
import jax.numpy as jnp
from jax import lax
from jax.sharding import PartitionSpec as P


def slot_numbers(chosen_ids, experts, capacity):
    flat_ids = chosen_ids.reshape(-1)
    labels = jnp.arange(experts, dtype=jnp.int32)
    onehot = (flat_ids[:, None] == labels[None, :]).astype(jnp.int32)
    before = jnp.cumsum(onehot, axis=0) - onehot
    position = jnp.sum(before * onehot, axis=1)
    return (flat_ids * capacity + position).reshape(chosen_ids.shape)


def route_matrix(slots, count):
    targets = jnp.arange(count, dtype=jnp.int32)
    return jnp.any(targets[:, None, None] == slots[None, :, :], axis=2).astype(jnp.bfloat16)


def on_device(tokens, expert_ids, gate_levels, gate_weight, up_weight, down_weight):
    tok_dev = tokens.shape[0]
    picks = expert_ids.shape[1]
    exp_dev = gate_weight.shape[0]
    n_expert = lax.axis_size("expert")
    experts = exp_dev * n_expert
    capacity = min(tok_dev, max(2, 2 * tok_dev * picks // experts))
    slot_count = experts * capacity
    own_slots = slot_numbers(expert_ids, experts, capacity)
    route = route_matrix(own_slots, slot_count)
    whole = lax.all_gather(tokens, "dp", axis=1, tiled=True)
    outgoing = jnp.dot(route, whole, preferred_element_type=jnp.float32).astype(jnp.bfloat16)
    outgoing = outgoing.reshape(n_expert, exp_dev, capacity, whole.shape[1])
    arrived = lax.all_to_all(outgoing, "expert", split_axis=0, concat_axis=0, tiled=True)
    gate_part = jnp.einsum(
        "sxcd,xdf->sxcf", arrived, gate_weight, preferred_element_type=jnp.float32
    )
    up_part = jnp.einsum("sxcd,xdf->sxcf", arrived, up_weight, preferred_element_type=jnp.float32)
    hidden = (jax.nn.silu(gate_part) * up_part).astype(jnp.bfloat16)
    out_features = down_weight.shape[2]
    outputs = jnp.einsum(
        "sxcf,xfk->sxck",
        lax.all_gather(hidden, "dp", axis=3, tiled=True),
        down_weight,
        preferred_element_type=jnp.float32,
    )
    result = outputs.astype(jnp.bfloat16)
    returned = lax.all_to_all(result, "expert", split_axis=0, concat_axis=0, tiled=True)
    returned = returned.reshape(slot_count, out_features)
    shares = gate_levels.astype(jnp.float32) / 256.0
    targets = jnp.arange(slot_count, dtype=jnp.int32)
    weighting = jnp.sum(
        jnp.where(
            targets[None, :, None] == own_slots[:, None, :], shares[:, None, :], jnp.float32(0.0)
        ),
        axis=2,
    )
    weighting = weighting.astype(jnp.bfloat16)
    combined = jnp.dot(weighting, returned, preferred_element_type=jnp.float32)
    return combined.astype(jnp.bfloat16)


def solution(mesh):
    in_specs = (
        P(("groups", "expert"), "dp"),
        P(("groups", "expert"), None),
        P(("groups", "expert"), None),
        P("expert", None, "dp"),
        P("expert", None, "dp"),
        P("expert", None, "dp"),
    )
    out_specs = P(("groups", "expert"), "dp")
    return jax.shard_map(
        on_device, mesh=mesh, in_specs=in_specs, out_specs=out_specs, check_vma=False
    )
```

profile of v0, /device:TPU:0, one launch (start us, length us, event | category | flops | bytes accessed | tf_op | source)
XLA Modules:
  0.0 241.4 jit_solution(17744205040662272902)
XLA Ops:
  6.5 0.0 all-gather.2.cloned.1.call-start
  6.5 0.8 copy.37
  7.3 0.1 eq.56
  7.4 0.1 eq.52
  7.5 1.2 reduce-window.6
  8.7 0.2 slice_reduce_fusion
  8.9 0.1 fusion.22
  9.0 0.1 reduce_sum.21
  9.1 0.1 copy.40
  9.2 0.7 multiply_add_fusion
  9.9 0.1 copy.41
  10.0 0.7 fusion.12
  10.7 7.4 %all_gather.6 = bf16[64,2048]{1,0:T(8,128)(2,1)S(1)} all-gather(bf16[64,1024]{1,0:T(8,128)(2,1)} %param.6), channel_id=1, replica_groups=mesh['groups'=2,'expert'=8,'dp'=2] {'dp'}, dimensions={1}, use_global_device_ids=true | all-gather | bytes 393216 | tf_op jit(solution)/shard_map/all_gather | solution.py:31
  18.1 1.3 convolution_convert_fusion
  19.4 0.0 slice-start.1
  19.4 0.0 slice-start.2
  19.4 99.1 %all_to_all.10 = bf16[8,2,64,2048]{3,2,1,0:T(8,128)(2,1)S(1)} all-to-all(bf16[8,2,64,2048]{3,2,1,0:T(8,128)(2,1)S(1)} %bitcast.64), channel_id=1, replica_groups=mesh['groups'=2,'expert'=8,'dp'=2] {'expert'}, dimensions={0} | all-to-all | bytes 8388608 | tf_op jit(solution)/shard_map/all_to_all | solution.py:34
  118.5 0.0 slice-done
  118.5 0.0 slice-done.1
  118.5 3.5 %fusion.2 = f32[2,8,64,768]{3,2,1,0:T(8,128)S(1)} fusion(bf16[2,2048,768]{2,1,0:T(8,128)(2,1)S(1)} %bitcast.67, bf16[8,2,64,2048]{3,2,1,0:T(8,128)(2,1)S(1)} %all_to_all.10), kind=kOutput, calls=%fused_computation.2 | convolution fusion | flops 3221225472 | bytes 13631488 | tf_op jit(solution)/shard_map/sxcd,xdf->sxcf/dot_general | solution.py:38
  122.0 0.0 slice-done.2
  122.0 4.9 %fusion.8 = bf16[8,2,64,768]{3,2,0,1:T(8,128)(2,1)} fusion(f32[2,8,64,768]{3,2,1,0:T(8,128)S(1)} %fusion.2, bf16[2,2048,768]{2,1,0:T(8,128)(2,1)S(1)} %bitcast.69, bf16[8,2,64,2048]{3,2,1,0:T(8,128)(2,1)S(1)} %all_to_all.10), kind=kOutput, calls=%fused_computation.10 | convolution fusion | flops 3225944064 | bytes 15204352 | tf_op jit(solution)/shard_map/sxcd,xdf->sxcf/dot_general | solution.py:35
  126.9 0.0 all-gather.2.cloned.1.call-update
  126.9 44.0 %all-gather.2.cloned.1.call-done = bf16[8,2,64,1536]{3,2,0,1:T(8,128)(2,1)} async-done(((bf16[8,2,64,768]{3,2,0,1:T(8,128)(2,1)}), bf16[8,2,64,1536]{3,2,0,1:T(8,128)(2,1)}) %all-gather.2.cloned.1.call-update) | async-done | bytes 3145744 | tf_op jit(solution)/shard_map/all_gather | solution.py:43
  170.9 7.2 %convert_bitcast_fusion = bf16[8,2,64,1024]{3,2,0,1:T(8,128)(2,1)S(1)} fusion(bf16[8,2,64,1536]{3,2,0,1:T(8,128)(2,1)} %all-gather.2.cloned.1.call-done, bf16[2,1536,1024]{2,1,0:T(8,128)(2,1)} %param.11), kind=kOutput, calls=%fused_computation.16 | convolution fusion | flops 3222274048 | bytes 11534336 | tf_op jit(solution)/shard_map/sxcf,xfk->sxck/dot_general | solution.py:41
  178.1 1.6 copy.46
  179.6 4.7 %all-to-all-start.1 = ((bf16[8,2,64,1024]{3,2,1,0:T(8,128)(2,1)}), bf16[8,2,64,1024]{3,2,1,0:T(8,128)(2,1)S(1)}, u32[]{:S(2)}, u32[]{:S(2)}) async-start(bf16[8,2,64,1024]{3,2,1,0:T(8,128)(2,1)} %copy.46), calls=%async_computation.1 | async-start | bytes 4194304 | tf_op jit(solution)/shard_map/all_to_all | solution.py:48
  184.4 0.0 copy-done
  184.4 0.1 copy.42
  184.5 0.7 select_reduce_fusion
  185.2 48.2 %all-to-all-done.1 = bf16[8,2,64,1024]{3,2,1,0:T(8,128)(2,1)S(1)} async-done(((bf16[8,2,64,1024]{3,2,1,0:T(8,128)(2,1)}), bf16[8,2,64,1024]{3,2,1,0:T(8,128)(2,1)S(1)}, u32[]{:S(2)}, u32[]{:S(2)}) %all-to-all-start.1) | async-done | bytes 2097184 | tf_op jit(solution)/shard_map/all_to_all | solution.py:48
  233.4 1.1 convolution_convert_fusion.1
  (10 shorter events, 0.1 us)
Async XLA Ops:
  6.5 164.4 %all-gather.2.cloned.1.call-start = ((), (), s32[]{:S(2)}) async-start(), calls=%async_computation.2 | async-start | bytes 4718592 | tf_op jit(solution)/shard_map/all_gather | solution.py:43
  18.1 100.4 %slice-start = ((s8[6291456]{0:T(1024)(128)(4,1)}), s8[4194304]{0:T(1024)(128)(4,1)S(1)}, s32[]{:S(2)}) async-start(s8[6291456]{0:T(1024)(128)(4,1)} %bitcast.66), calls=%async_computation.3 | async-start | bytes 8388608
  19.4 99.1 %slice-start.1 = ((s8[6291456]{0:T(1024)(128)(4,1)}), s8[2097152]{0:T(1024)(128)(4,1)S(1)}, s32[]{:S(2)}) async-start(s8[6291456]{0:T(1024)(128)(4,1)} %bitcast.66), calls=%async_computation.4 | async-start | bytes 4194304
  19.4 102.6 %slice-start.2 = ((s8[6291456]{0:T(1024)(128)(4,1)}), s8[4194304]{0:T(1024)(128)(4,1)S(1)}, s32[]{:S(2)}) async-start(s8[6291456]{0:T(1024)(128)(4,1)} %bitcast.68), calls=%async_computation.5 | async-start | bytes 8388608
  118.5 3.5 %slice-start.3 = ((s8[6291456]{0:T(1024)(128)(4,1)}), s8[2097152]{0:T(1024)(128)(4,1)S(1)}, s32[]{:S(2)}) async-start(s8[6291456]{0:T(1024)(128)(4,1)} %bitcast.68), calls=%async_computation.6 | async-start | bytes 4194304
  179.6 4.7 %copy-start = (s32[64,8]{0,1:T(8,128)S(1)}, s32[64,8]{0,1:T(8,128)}, u32[]{:S(2)}) copy-start(s32[64,8]{0,1:T(8,128)} %param.8) | copy-start | bytes 6148
  179.6 53.8 %all-to-all-start.1 = ((bf16[8,2,64,1024]{3,2,1,0:T(8,128)(2,1)}), bf16[8,2,64,1024]{3,2,1,0:T(8,128)(2,1)S(1)}, u32[]{:S(2)}, u32[]{:S(2)}) async-start(bf16[8,2,64,1024]{3,2,1,0:T(8,128)(2,1)} %copy.46), calls=%async_computation.1 | async-start | bytes 4194304 | tf_op jit(solution)/shard_map/all_to_all | solution.py:48
Sparse Core Ops, SparseCore 0:
  127.0 43.8 all-gather.1
where the time goes:
time: 242 us; the launch traced here: 241 us
  blocking collectives  107 us (44%)
  waiting for transfers between devices  92.2 us (38%)
  matrix products  17.9 us (7%)
  between operations  13.5 us (6%)
  starting transfers between devices  4.74 us (2%)
  other arithmetic  3.42 us (1%)
  local copies, waits for them, and re-layouts  3.08 us (1%)
    all_to_all x1, blocking collectives, on_device(): lax.all_to_all(outgoing, 'expert', split_axis=0, concat_axis=0, tiled=True)  99.1 us
    all_to_all x1, waiting for transfers between devices, on_device(): lax.all_to_all(result, 'expert', split_axis=0, concat_axis=0, tiled=True)  48.2 us
    all_gather x1, waiting for transfers between devices, on_device(): lax.all_gather(hidden, 'dp', axis=3, tiled=True)  44 us
    all_gather x1, blocking collectives, on_device(): whole = lax.all_gather(tokens, 'dp', axis=1, tiled=True)  7.39 us
    dot_general x1, matrix products, on_device(): jnp.einsum('sxcf,xfk->sxck', lax.all_gather(hidden, 'dp', axis=3, tiled=T...  7.15 us
    dot_general x1, matrix products, on_device(): jnp.einsum('sxcd,xdf->sxcf', arrived, gate_weight, preferred_element_type...  4.87 us
  transfers between devices with their start and end apart: 2, of which 2 were waited for; matrix products, arithmetic and copies ran while one was open for 0% of the time, Pallas kernels for 0%

commit v1 on v0

--- a/solution.py
+++ b/solution.py
@@ -40,7 +40,7 @@
     out_features = down_weight.shape[2]
     outputs = jnp.einsum(
         "sxcf,xfk->sxck",
-        lax.all_gather(hidden, "dp", axis=3, tiled=True),
+        jnp.concatenate(lax.all_gather(hidden, "dp"), axis=3),
         down_weight,
         preferred_element_type=jnp.float32,
     )

time: 242 us -> 243 us (level)
  no operation moved by 1% of the time
where the time goes in v1:
time: 243 us
  blocking collectives  107 us (44%)
  waiting for transfers between devices  92.2 us (38%)
  matrix products  17.4 us (7%)
  between operations  13.5 us (6%)
  local copies, waits for them, and re-layouts  5.23 us (2%)
  starting transfers between devices  4.74 us (2%)
  other arithmetic  3.42 us (1%)
    all_to_all x1, blocking collectives, on_device(): lax.all_to_all(outgoing, 'expert', split_axis=0, concat_axis=0, tiled=True)  99.1 us
    all_to_all x1, waiting for transfers between devices, on_device(): lax.all_to_all(result, 'expert', split_axis=0, concat_axis=0, tiled=True)  48.2 us
    all_gather x1, waiting for transfers between devices, on_device(): lax.all_gather(hidden, 'dp')  44 us
    all_gather x1, blocking collectives, on_device(): whole = lax.all_gather(tokens, 'dp', axis=1, tiled=True)  7.39 us
    dot_general x1, matrix products, on_device(): jnp.einsum('sxcf,xfk->sxck', jnp.concatenate(lax.all_gather(hidden, 'dp')...  6.64 us
    dot_general x1, matrix products, on_device(): jnp.einsum('sxcd,xdf->sxcf', arrived, gate_weight, preferred_element_type...  4.87 us
  transfers between devices with their start and end apart: 2, of which 2 were waited for; matrix products, arithmetic and copies ran while one was open for 0% of the time, Pallas kernels for 0%

profile of v1, /device:TPU:0, one launch (start us, length us, event | category | flops | bytes accessed | tf_op | source)
XLA Modules:
  0.0 243.0 jit_solution(3764335375071208673)
XLA Ops:
  6.5 0.0 all-gather.3.cloned.1.call-start
  6.5 0.8 copy.41
  7.3 0.1 eq.56
  7.4 0.1 eq.52
  7.5 1.2 reduce-window.6
  8.7 0.2 slice_reduce_fusion
  8.9 0.1 fusion.22
  9.0 0.1 reduce_sum.21
  9.1 0.1 copy.44
  9.2 0.7 multiply_add_fusion
  9.9 0.1 copy.45
  10.0 0.7 fusion.12
  10.7 7.4 %all_gather.9 = bf16[64,2048]{1,0:T(8,128)(2,1)S(1)} all-gather(bf16[64,1024]{1,0:T(8,128)(2,1)} %param.6), channel_id=1, replica_groups=mesh['groups'=2,'expert'=8,'dp'=2] {'dp'}, dimensions={1}, use_global_device_ids=true | all-gather | bytes 393216 | tf_op jit(solution)/shard_map/all_gather | solution.py:31
  18.1 1.3 convolution_convert_fusion
  19.4 0.0 slice-start.1
  19.4 0.0 slice-start.2
  19.4 99.1 %all_to_all.10 = bf16[8,2,64,2048]{3,2,1,0:T(8,128)(2,1)S(1)} all-to-all(bf16[8,2,64,2048]{3,2,1,0:T(8,128)(2,1)S(1)} %bitcast.69), channel_id=1, replica_groups=mesh['groups'=2,'expert'=8,'dp'=2] {'expert'}, dimensions={0} | all-to-all | bytes 8388608 | tf_op jit(solution)/shard_map/all_to_all | solution.py:34
  118.5 0.0 slice-done
  118.5 0.0 slice-done.1
  118.5 3.5 %fusion.2 = f32[2,8,64,768]{3,2,1,0:T(8,128)S(1)} fusion(bf16[2,2048,768]{2,1,0:T(8,128)(2,1)S(1)} %bitcast.74, bf16[8,2,64,2048]{3,2,1,0:T(8,128)(2,1)S(1)} %all_to_all.10), kind=kOutput, calls=%fused_computation.2 | convolution fusion | flops 3221225472 | bytes 13631488 | tf_op jit(solution)/shard_map/sxcd,xdf->sxcf/dot_general | solution.py:38
  122.0 0.0 slice-done.2
  122.0 4.9 %fusion.8 = bf16[8,2,64,768]{3,2,0,1:T(8,128)(2,1)} fusion(f32[2,8,64,768]{3,2,1,0:T(8,128)S(1)} %fusion.2, bf16[2,2048,768]{2,1,0:T(8,128)(2,1)S(1)} %bitcast.76, bf16[8,2,64,2048]{3,2,1,0:T(8,128)(2,1)S(1)} %all_to_all.10), kind=kOutput, calls=%fused_computation.10 | convolution fusion | flops 3225944064 | bytes 15204352 | tf_op jit(solution)/shard_map/sxcd,xdf->sxcf/dot_general | solution.py:35
  126.9 0.0 all-gather.3.cloned.1.call-update
  126.9 44.0 %all-gather.3.cloned.1.call-done = bf16[16,2,64,768]{3,2,0,1:T(8,128)(2,1)} async-done(((bf16[8,2,64,768]{3,2,0,1:T(8,128)(2,1)}), bf16[16,2,64,768]{3,2,0,1:T(8,128)(2,1)}) %all-gather.3.cloned.1.call-update) | async-done | bytes 3145744 | tf_op jit(solution)/shard_map/all_gather | solution.py:43
  170.9 2.2 copy.56
  173.1 6.6 %convert_bitcast_fusion = bf16[8,2,64,1024]{3,2,0,1:T(8,128)(2,1)S(1)} fusion(bf16[8,2,64,1536]{3,2,0,1:T(8,128)(2,1)S(1)} %bitcast.72, bf16[2,1536,1024]{2,1,0:T(8,128)(2,1)} %param.11), kind=kOutput, calls=%fused_computation.16 | convolution fusion | flops 3222274048 | bytes 11534336 | tf_op jit(solution)/shard_map/sxcf,xfk->sxck/dot_general | solution.py:41
  179.7 1.6 copy.51
  181.3 4.7 %all-to-all-start.1 = ((bf16[8,2,64,1024]{3,2,1,0:T(8,128)(2,1)}), bf16[8,2,64,1024]{3,2,1,0:T(8,128)(2,1)S(1)}, u32[]{:S(2)}, u32[]{:S(2)}) async-start(bf16[8,2,64,1024]{3,2,1,0:T(8,128)(2,1)} %copy.51), calls=%async_computation.1 | async-start | bytes 4194304 | tf_op jit(solution)/shard_map/all_to_all | solution.py:48
  186.0 0.1 copy.46
  186.1 0.7 select_reduce_fusion
  186.8 48.2 %all-to-all-done.1 = bf16[8,2,64,1024]{3,2,1,0:T(8,128)(2,1)S(1)} async-done(((bf16[8,2,64,1024]{3,2,1,0:T(8,128)(2,1)}), bf16[8,2,64,1024]{3,2,1,0:T(8,128)(2,1)S(1)}, u32[]{:S(2)}, u32[]{:S(2)}) %all-to-all-start.1) | async-done | bytes 2097184 | tf_op jit(solution)/shard_map/all_to_all | solution.py:48
  235.0 1.1 convolution_convert_fusion.1
  (11 shorter events, 0.1 us)
Async XLA Ops:
  6.5 164.4 %all-gather.3.cloned.1.call-start = ((), (), s32[]{:S(2)}) async-start(), calls=%async_computation.2 | async-start | bytes 4718592 | tf_op jit(solution)/shard_map/all_gather | solution.py:43
  18.1 100.4 %slice-start = ((s8[6291456]{0:T(1024)(128)(4,1)}), s8[4194304]{0:T(1024)(128)(4,1)S(1)}, s32[]{:S(2)}) async-start(s8[6291456]{0:T(1024)(128)(4,1)} %bitcast.73), calls=%async_computation.3 | async-start | bytes 8388608
  19.4 99.1 %slice-start.1 = ((s8[6291456]{0:T(1024)(128)(4,1)}), s8[2097152]{0:T(1024)(128)(4,1)S(1)}, s32[]{:S(2)}) async-start(s8[6291456]{0:T(1024)(128)(4,1)} %bitcast.73), calls=%async_computation.4 | async-start | bytes 4194304
  19.4 102.6 %slice-start.2 = ((s8[6291456]{0:T(1024)(128)(4,1)}), s8[4194304]{0:T(1024)(128)(4,1)S(1)}, s32[]{:S(2)}) async-start(s8[6291456]{0:T(1024)(128)(4,1)} %bitcast.75), calls=%async_computation.5 | async-start | bytes 8388608
  118.5 3.5 %slice-start.3 = ((s8[6291456]{0:T(1024)(128)(4,1)}), s8[2097152]{0:T(1024)(128)(4,1)S(1)}, s32[]{:S(2)}) async-start(s8[6291456]{0:T(1024)(128)(4,1)} %bitcast.75), calls=%async_computation.6 | async-start | bytes 4194304
  181.3 4.7 %copy-start = (s32[64,8]{0,1:T(8,128)S(1)}, s32[64,8]{0,1:T(8,128)}, u32[]{:S(2)}) copy-start(s32[64,8]{0,1:T(8,128)} %param.8) | copy-start | bytes 6148
  181.3 53.8 %all-to-all-start.1 = ((bf16[8,2,64,1024]{3,2,1,0:T(8,128)(2,1)}), bf16[8,2,64,1024]{3,2,1,0:T(8,128)(2,1)S(1)}, u32[]{:S(2)}, u32[]{:S(2)}) async-start(bf16[8,2,64,1024]{3,2,1,0:T(8,128)(2,1)} %copy.51), calls=%async_computation.1 | async-start | bytes 4194304 | tf_op jit(solution)/shard_map/all_to_all | solution.py:48
Sparse Core Ops, SparseCore 0:
  127.0 43.8 all-gather.2
